TPU v7x, 32 devices: a whole 2x2x4 slice. The times are simulated.
32 devices in a mesh: state: 2 (over x), bond: 16 (over z, y, core).
Axes of the slice: x: 2, y: 2, z: 4, core: 2. Of those that a mesh axis runs over, the one named last changes fastest.
Arguments:
- intersect_left: bfloat16 [2, 2048, 2048], P('state', 'bond'), may hold values from -0.125 to 0.125
- stored_block: bfloat16 [2, 4, 2048, 2048], P('state', None, 'bond'), may hold values from -6 to 6
- stored_site: bfloat16 [2, 2, 2048, 2048], P('state', None, 'bond'), may hold values from -6 to 6
- current_site: bfloat16 [2048, 2, 2048], P('bond', None, 'state'), may hold values from -0.09375 to 0.09375
- current_block: bfloat16 [4, 2048, 2048], P(None, 'bond', 'state'), may hold values from -6 to 6
- penalty_weight: float32 [2], replicated, may hold values from 0.5 to 4
Outputs:
- penalized: float32 [4, 2048, 2048], P(None, 'bond', 'state')
- intersect_next: bfloat16 [2, 2048, 2048], P('state', 'bond')
All inputs are finite; a program needn't handle non-finite values.
Results may differ from a plain program's by a relative error of at most 0.0055.
Values may be sent and summed in bfloat16 or wider, within the bound.
A program may use at most 64 MiB of HBM per device.

v0:
```python
import functools

import jax
import jax.numpy as jnp
from jax import lax
from jax.experimental import pallas as pl
from jax.experimental.pallas import tpu as pltpu
from jax.sharding import PartitionSpec as P

MESH = pl.DeviceIdType.MESH
CORES = 2
TILE = 256


def kernel(
    states, bonds, rows_y,
    env_hbm, block_hbm, site_hbm, grow_hbm, current_hbm, weight_ref,
    pen_hbm, next_hbm,
    ebuf, abuf, stored, cbuf, psend, precv, mbuf, acc, pen, nsend, nrecv, iall,
    local_sem, out_sem, e_send, e_recv, a_send, a_recv, p_send, p_recv, m_send, m_recv,
    i_send, i_recv, n_send, n_recv, c_send, c_recv, line,
):
    nc, ny = CORES, rows_y
    nz = bonds // (nc * ny)
    rows, width = ebuf.shape[1:]
    pairs = block_hbm.shape[0]
    phys = site_hbm.shape[0]
    w = block_hbm.shape[1]
    per_group = TILE // rows
    per_row = ny * nc * rows // TILE
    groups = width // TILE
    gpp = groups // states
    fwidth = abuf.shape[2] // phys
    nfb = fwidth // w
    count = states * bonds

    k = lax.axis_index("state")
    me = lax.axis_index("bond")
    c = lax.rem(me, nc)
    y = lax.rem(lax.div(me, nc), ny)
    z = lax.div(me, nc * ny)
    flat = k * bonds + me

    def slot(zz, yy, cc):
        return (zz * ny + yy) * nc + cc

    e_load = pltpu.make_async_copy(env_hbm, ebuf.at[me], local_sem.at[0])
    a_load = pltpu.make_async_copy(grow_hbm, abuf.at[me], local_sem.at[1])
    e_load.start()
    c_loads = [
        pltpu.make_async_copy(
            current_hbm.at[:, :, pl.ds(g * TILE, TILE)], cbuf.at[k * gpp + g], local_sem.at[3]
        )
        for g in range(gpp)
    ]
    for copy in c_loads:
        copy.start()
    loads = []
    for q in range(pairs):
        loads.append(pltpu.make_async_copy(block_hbm.at[q], stored.at[pl.ds(q * w, w)], local_sem.at[2]))
    for s in range(phys):
        loads.append(
            pltpu.make_async_copy(site_hbm.at[s], stored.at[pl.ds((pairs + s) * w, w)], local_sem.at[2])
        )
    for copy in loads:
        copy.start()
    a_load.start()

    barrier = pltpu.get_barrier_semaphore()

    @pl.loop(1, count)
    def _(r):
        peer = lax.rem(flat + r, count)
        pl.semaphore_signal(
            barrier, inc=1, device_id=(lax.div(peer, bonds), lax.rem(peer, bonds)), device_id_type=MESH
        )

    pl.semaphore_wait(barrier, count - 1)

    env = (ebuf, e_send, e_recv)
    site = (abuf, a_send, a_recv)

    def copy_of(what, blk, dest):
        buf, ss, rs = what
        return pltpu.make_async_remote_copy(
            src_ref=buf.at[blk], dst_ref=buf.at[blk], send_sem=ss, recv_sem=rs.at[blk],
            device_id=(k, dest), device_id_type=MESH,
        )

    def act(what, blk, dest, drain):
        copy = copy_of(what, blk, dest)
        if drain:
            copy.wait_send()
        else:
            copy.start()

    def arrive(what, blk):
        copy_of(what, blk, me).wait_recv()

    def spread(what, blk, drain):
        @pl.when(y > 0)
        def _():
            act(what, blk, slot(z, y - 1, c), drain)

        @pl.when(y < ny - 1)
        def _():
            act(what, blk, slot(z, y + 1, c), drain)

        act(what, blk, slot(z, y, 1 - c), drain)

    def column(what, i, drain=False):
        if i == 0:
            blk = slot(z, y, c)

            @pl.when(z > 0)
            def _():
                act(what, blk, slot(z - 1, y, c), drain)

            @pl.when(z < nz - 1)
            def _():
                act(what, blk, slot(z + 1, y, c), drain)

            spread(what, blk, drain)
            return
        for sign in (1, -1):
            zz = z - sign * i
            onward = z + sign

            @pl.when(jnp.logical_and(zz >= 0, zz < nz))
            def _():
                blk = slot(zz, y, c)
                if not drain:
                    arrive(what, blk)

                @pl.when(jnp.logical_and(onward >= 0, onward < nz))
                def _():
                    act(what, blk, slot(onward, y, c), drain)

                spread(what, blk, drain)

    def turn(j):
        least = jnp.minimum(z, nz - 1 - z)
        near = (j + 1) // 2
        inner = z - near if j % 2 else z + near
        far = j - least
        outer = jnp.where(z <= nz - 1 - z, z + far, z - far)
        return jnp.where(j <= 2 * least, inner, outer)

    def across(what, j, drain=False):
        zz = turn(j)
        for u in range(1, ny):
            for sign in (1, -1):
                yy = y - sign * u
                onward = y + sign

                @pl.when(jnp.logical_and(yy >= 0, yy < ny))
                def _():
                    blk = slot(zz, yy, c)
                    if not drain:
                        arrive(what, blk)

                    @pl.when(jnp.logical_and(onward >= 0, onward < ny))
                    def _():
                        act(what, blk, slot(z, onward, c), drain)

                    act(what, blk, slot(z, y, 1 - c), drain)

    def sibling(what, j):
        zz = turn(j)
        for yy in range(ny):
            arrive(what, slot(zz, yy, 1 - c))

    def p_copy(g, peer):
        return pltpu.make_async_remote_copy(
            src_ref=psend.at[g], dst_ref=precv.at[k, lax.rem(g, gpp)], send_sem=p_send,
            recv_sem=p_recv.at[k], device_id=(peer, me), device_id_type=MESH,
        )

    def m_copy(g, peer):
        return pltpu.make_async_remote_copy(
            src_ref=mbuf.at[g, :, k], dst_ref=mbuf.at[g, :, k], send_sem=m_send,
            recv_sem=m_recv.at[k], device_id=(peer, me), device_id_type=MESH,
        )

    def c_copy(zz, peer):
        part = pl.ds(zz * per_row, per_row)
        return pltpu.make_async_remote_copy(
            src_ref=cbuf.at[part], dst_ref=cbuf.at[part], send_sem=c_send, recv_sem=c_recv.at[zz],
            device_id=(peer, me), device_id_type=MESH,
        )

    def share(drain=False):
        for j in range(nz):
            zz = turn(j)

            @pl.when(lax.div(zz * per_row, gpp) == k)
            def _():
                for other in range(1, states):
                    copy = c_copy(zz, lax.rem(k + other, states))
                    if drain:
                        copy.wait_send()
                    else:
                        copy.start()

    def project(j):
        zz = turn(j)

        @pl.when(lax.div(zz * per_row, gpp) != k)
        def _():
            c_copy(zz, k).wait_recv()

        @pl.loop(0, per_row)
        def _(r):
            g = zz * per_row + r
            left = ebuf[pl.ds(g * per_group, per_group)].reshape(TILE, width)
            prod = lax.dot_general(
                stored[...], left, (((1,), (1,)), ((), ())), preferred_element_type=jnp.float32
            )
            mbuf[g, :, k] = prod[pairs * w :].astype(jnp.bfloat16).reshape(phys, w, TILE)
            whole = prod[: pairs * w]
            here = cbuf[g].reshape(pairs * w, TILE).astype(jnp.float32)
            line[...] += jnp.sum((whole * here).reshape(pairs * w // 8, 8, TILE), axis=0)
            part = whole.astype(jnp.bfloat16)
            psend[g] = part
            owner = lax.div(g, gpp)

            @pl.when(owner == k)
            def _():
                precv[k, lax.rem(g, gpp)] = part

            for other in range(1, states):
                peer = lax.rem(k + other, states)

                m_copy(g, peer).start()

                @pl.when(owner == peer)
                def _():
                    p_copy(g, peer).start()

    def grow(j):
        zz = turn(j)

        @pl.loop(0, per_row)
        def _(r):
            g = zz * per_row + r
            right = abuf[pl.ds(g * per_group, per_group)].reshape(TILE, phys * fwidth)
            total = jnp.zeros((states * w, fwidth), jnp.float32)
            for s in range(phys):
                total = total + jnp.dot(
                    mbuf[g, s].reshape(states * w, TILE),
                    right[:, s * fwidth : (s + 1) * fwidth],
                    preferred_element_type=jnp.float32,
                )
            acc[...] += total

    def overlap():
        short = jnp.sum(line[...], axis=0, keepdims=True)
        total = short[:, :128]
        for at in range(128, TILE, 128):
            total = total + short[:, at : at + 128]
        iall[flat] = total

    def i_copy(peer):
        return pltpu.make_async_remote_copy(
            src_ref=iall.at[flat], dst_ref=iall.at[flat], send_sem=i_send, recv_sem=i_recv,
            device_id=(lax.div(peer, bonds), lax.rem(peer, bonds)), device_id_type=MESH,
        )

    def tell():
        @pl.loop(1, count)
        def _(r):
            i_copy(lax.rem(flat + r, count)).start()

    pen_copies = [
        pltpu.make_async_copy(pen.at[g], pen_hbm.at[:, :, pl.ds(g * TILE, TILE)], out_sem.at[0])
        for g in range(gpp)
    ]

    def penalize():
        rest = iall.at[pl.ds(0, count - 1)]
        pltpu.make_async_remote_copy(
            src_ref=rest, dst_ref=rest, send_sem=i_send, recv_sem=i_recv,
            device_id=(k, me), device_id_type=MESH,
        ).wait_recv()
        for other in range(1, states):
            peer = lax.rem(k + other, states)
            pltpu.make_async_remote_copy(
                src_ref=precv.at[peer], dst_ref=precv.at[peer], send_sem=p_send,
                recv_sem=p_recv.at[peer], device_id=(peer, me), device_id_type=MESH,
            ).wait_recv()
        scale = 1.0 / (phys * width)
        factors = [
            weight_ref[kk] * (jnp.sum(iall[kk * bonds : (kk + 1) * bonds]) * scale)
            for kk in range(states)
        ]
        for g in range(gpp):
            value = cbuf[k * gpp + g].reshape(pairs * w, TILE).astype(jnp.float32)
            for kk in range(states):
                value = value + factors[kk] * precv[kk, g].astype(jnp.float32)
            pen[g] = value.reshape(pairs, w, TILE)
            pen_copies[g].start()

    acc[...] = jnp.zeros_like(acc)
    line[...] = jnp.zeros_like(line)
    e_load.wait()
    for i in range(2 * nz):
        if i < nz:
            column(env, i)
        if i == 0:
            for copy in c_loads:
                copy.wait()
            share()
        if i >= nz - 1 and i - (nz - 1) < nz:
            if i == nz - 1:
                a_load.wait()
            column(site, i - (nz - 1))
        if 1 <= i <= nz:
            across(env, i - 1)
            sibling(env, i - 1)
            if i == 1:
                for copy in loads:
                    copy.wait()
            project(i - 1)
            if i == nz:
                overlap()
                tell()
        if i >= nz:
            across(site, i - nz)
            sibling(site, i - nz)
            if i == nz:
                for other in range(1, states):
                    peer = lax.rem(k + other, states)
                    mine = mbuf.at[:, :, peer]
                    pltpu.make_async_remote_copy(
                        src_ref=mine, dst_ref=mine, send_sem=m_send, recv_sem=m_recv.at[peer],
                        device_id=(peer, me), device_id_type=MESH,
                    ).wait_recv()
            grow(i - nz)
            if i == min(nz + 1, 2 * nz - 1):
                penalize()

    def n_copy(kk, fb):
        return pltpu.make_async_remote_copy(
            src_ref=nsend.at[kk, fb], dst_ref=nrecv.at[me], send_sem=n_send, recv_sem=n_recv,
            device_id=(kk, k * nfb + fb), device_id_type=MESH,
        )

    def is_me(kk, fb):
        return jnp.logical_and(k == kk, me == k * nfb + fb)

    for kk in range(states):
        for fb in range(nfb):
            part = acc[kk * w : (kk + 1) * w, fb * w : (fb + 1) * w].T.astype(jnp.bfloat16)
            nsend[kk, fb] = part

            @pl.when(is_me(kk, fb))
            def _():
                nrecv[me] = part

            @pl.when(jnp.logical_not(is_me(kk, fb)))
            def _():
                n_copy(kk, fb).start()

    inside = lax.div(me, nfb) == k

    def all_of(number):
        rest = nrecv.at[pl.ds(0, number)]
        return pltpu.make_async_remote_copy(
            src_ref=rest, dst_ref=rest, send_sem=n_send, recv_sem=n_recv,
            device_id=(k, me), device_id_type=MESH,
        )

    for i in range(nz):
        for what in (env, site):
            column(what, i, drain=True)
            across(what, i, drain=True)

    share(drain=True)

    @pl.loop(0, groups)
    def _(g):
        for other in range(1, states):
            peer = lax.rem(k + other, states)

            @pl.when(lax.div(g, gpp) == peer)
            def _():
                p_copy(g, peer).wait_send()

            m_copy(g, peer).wait_send()

    @pl.loop(1, count)
    def _(r):
        i_copy(lax.rem(flat + r, count)).wait_send()

    for copy in pen_copies:
        copy.wait()
    for kk in range(states):
        for fb in range(nfb):
            @pl.when(jnp.logical_not(is_me(kk, fb)))
            def _():
                n_copy(kk, fb).wait_send()

    @pl.when(inside)
    def _():
        all_of(bonds - 1).wait_recv()

    @pl.when(jnp.logical_not(inside))
    def _():
        all_of(bonds).wait_recv()

    store = pltpu.make_async_copy(nrecv, next_hbm, out_sem.at[1])
    store.start()
    store.wait()


def shards(states, bonds, intersect_left, stored_block, stored_site, current_site, current_block, penalty_weight):
    rows, width = intersect_left.shape[1:]
    pairs, w = stored_block.shape[1:3]
    phys = stored_site.shape[1]
    fwidth = current_site.shape[2]
    groups = width // TILE
    gpp = groups // states
    rows_y = 1
    while 4 * rows_y * rows_y <= bonds // CORES:
        rows_y *= 2
    bf, f32 = jnp.bfloat16, jnp.float32
    anywhere = pl.BlockSpec(memory_space=pl.ANY)
    dma = pltpu.SemaphoreType.DMA
    penalized, grown = pl.pallas_call(
        functools.partial(kernel, states, bonds, rows_y),
        out_shape=(
            jax.ShapeDtypeStruct(current_block.shape, f32),
            jax.ShapeDtypeStruct((bonds, w, w), bf),
        ),
        in_specs=[anywhere] * 5 + [pl.BlockSpec(memory_space=pltpu.SMEM)],
        out_specs=(anywhere, anywhere),
        scratch_shapes=[
            pltpu.VMEM((bonds, rows, width), bf),
            pltpu.VMEM((bonds, rows, phys * fwidth), bf),
            pltpu.VMEM(((pairs + phys) * w, width), bf),
            pltpu.VMEM((groups, pairs, w, TILE), bf),
            pltpu.VMEM((groups, pairs * w, TILE), bf),
            pltpu.VMEM((states, gpp, pairs * w, TILE), bf),
            pltpu.VMEM((groups, phys, states, w, TILE), bf),
            pltpu.VMEM((states * w, fwidth), f32),
            pltpu.VMEM((gpp, pairs, w, TILE), f32),
            pltpu.VMEM((states, fwidth // w, w, w), bf),
            pltpu.VMEM((bonds, w, w), bf),
            pltpu.VMEM((states * bonds, 1, 128), f32),
            dma((4,)), dma((2,)),
            dma, dma((bonds,)), dma, dma((bonds,)),
            dma, dma((states,)), dma, dma((states,)),
            dma, dma, dma, dma,
            dma, dma((bonds,)),
            pltpu.VMEM((8, TILE), f32),
        ],
        compiler_params=pltpu.CompilerParams(
            collective_id=0, has_side_effects=True, vmem_limit_bytes=60 * 1024 * 1024
        ),
    )(
        intersect_left[0], stored_block[0], stored_site[0],
        current_site.reshape(rows, phys * fwidth), current_block, penalty_weight,
    )
    return penalized, grown.transpose(1, 0, 2).reshape(1, w, bonds * w)


def solution(mesh):
    placed = (
        P("state", "bond", None),
        P("state", None, "bond", None),
        P("state", None, "bond", None),
        P("bond", None, "state"),
        P(None, "bond", "state"),
        P(),
    )
    return jax.shard_map(
        functools.partial(shards, mesh.shape["state"], mesh.shape["bond"]),
        mesh=mesh,
        in_specs=placed,
        out_specs=(P(None, "bond", "state"), P("state", "bond", None)),
        check_vma=False,
    )
```

profile of v0, /device:TPU:27, one launch (start us, length us, event | category | flops | bytes accessed | tf_op | source)
XLA Modules:
  0.0 133.6 jit_solution(3042384249193851340)
XLA Ops:
  0.6 2.0 %copy.10 = bf16[16,8,2,1024]{3,1,2,0:T(8,128)(2,1)} copy(bf16[16,8,2,1024]{3,2,1,0:T(2,128)(2,1)} %bitcast.11) | data formatting | bytes 1048576
  2.6 127.2 %shard_map.77 = (f32[4,128,1024]{2,1,0:T(8,128)}, bf16[16,128,128]{2,1,0:T(8,128)(2,1)}) custom-call(bf16[128,2048]{1,0:T(8,128)(2,1)} %bitcast.13, bf16[4,128,2048]{2,1,0:T(8,128)(2,1)} %bitcast.7, bf16[2,128,2048]{2,1,0:T(8,128)(2,1)} %bitcast.10, bf16[128,2048]{1,0:T(8,128)(2,1)} %bitcast.9, bf16[4,128,1024]{2,1,0:T(8,128)(2,1)} %current_hbm.1, f32[2]{0:T(128)} %weight_ref.1), custom_call_target="tpu_custom_call" | custom-call | tf_op jit(solution)/shard_map/pallas_call | solution.py:429
  129.8 0.0 copy-start
  129.8 1.5 %copy.8 = bf16[128,16,128]{0,2,1:T(8,128)(2,1)S(1)} copy(bf16[128,16,128]{2,0,1:T(8,128)(2,1)} %bitcast.12) | data formatting | bytes 1048576 | tf_op jit(solution)/shard_map/transpose | solution.py:464
  131.3 1.0 copy.9
  132.3 0.0 copy-done
  132.3 1.3 copy.12
Async XLA Ops:
  129.8 2.5 %copy-start = (f32[4,128,1024]{2,1,0:T(8,128)S(1)}, f32[4,128,1024]{2,1,0:T(8,128)}, u32[]{:S(2)}) copy-start(f32[4,128,1024]{2,1,0:T(8,128)} %get-tuple-element.10) | copy-start | bytes 6291460
where the time goes:
time: 134 us
  Pallas kernels  127 us (95%)
  local copies, waits for them, and re-layouts  5.75 us (4%)
    pallas_call x1, Pallas kernels, shards(): pl.pallas_call(functools.partial(kernel, states, bonds, rows_y), out_shap...  127 us
    unnamed x5, local copies, waits for them, and re-layouts  4.29 us

commit v1 on v0

v1 whole, which is shorter than its diff:
```python
import functools

import jax
import jax.numpy as jnp
from jax import lax
from jax.experimental import pallas as pl
from jax.experimental.pallas import tpu as pltpu
from jax.sharding import PartitionSpec as P

MESH = pl.DeviceIdType.MESH
CORES = 2
TILE = 256
PARTS = 2


def both(*conds):
    return functools.reduce(jnp.logical_and, conds)


def kernel(
    states, bonds, rows_y, fch,
    env_hbm, block_hbm, site_hbm, grow_hbm, current_hbm, weight_ref,
    pen_hbm, next_hbm,
    ebuf, abuf, stored, cbuf, psend, precv, mown, mbuf, acc, part, prt, nsend, nbuf, pen, iplane, iline, istate, line,
    local_sem, out_sem, e_send, e_recv, a_send, a_recv, p_send, p_recv, my_send, my_recv, mx_send, mx_recv,
    c_send, c_recv, i_send, i_recv, t_send, t_recv, r_send, r_recv, n_send, n_recv,
):
    nc, ny = CORES, rows_y
    nz = bonds // (nc * ny)
    hr, width = ebuf.shape[2:]
    rows = hr * PARTS
    pairs, w = block_hbm.shape[:2]
    phys = site_hbm.shape[0]
    fwidth = grow_hbm.shape[1] // phys
    nch = fwidth // fch
    bpc = fch // w
    fbs = fwidth // w
    mine = fbs // ny
    cell = nc * rows
    per_group = TILE // rows
    tpp = ny * cell // TILE
    cpt = TILE // cell
    groups = width // TILE
    gpp = groups // states
    count = states * bonds
    ecols = states * ny * w
    direct = w % 128 == 0
    piece = phys * cell

    k = lax.axis_index("state")
    me = lax.axis_index("bond")
    c = lax.rem(me, nc)
    y = lax.rem(lax.div(me, nc), ny)
    z = lax.div(me, nc * ny)
    flat = k * bonds + me
    near = ny * nc
    slices = PARTS * tpp

    def slot(zz, yy, cc):
        return (zz * ny + yy) * nc + cc

    sib = slot(z, y, 1 - c)

    def column_of(h, q):
        if direct:
            return (h // nc * ny + q) * nc + h % nc
        return h * bpc + q

    e_load = pltpu.make_async_copy(env_hbm, ebuf.at[me], local_sem.at[0])
    e_load.start()
    a_loads = []
    for h in range(nch):
        for s in range(phys):
            for q in range(bpc if direct else 1):
                size = w if direct else fch
                a_loads.append(
                    pltpu.make_async_copy(
                        grow_hbm.at[:, pl.ds(s * fwidth + column_of(h, q) * w, size)],
                        abuf.at[h, z, s, c, :, pl.ds(q * w, size)],
                        local_sem.at[1],
                    )
                )
    for copy in a_loads:
        copy.start()
    loads = []
    for q in range(pairs):
        loads.append(pltpu.make_async_copy(block_hbm.at[q], stored.at[pl.ds(q * w, w)], local_sem.at[2]))
    for s in range(phys):
        loads.append(
            pltpu.make_async_copy(site_hbm.at[s], stored.at[pl.ds((pairs + s) * w, w)], local_sem.at[2])
        )
    for copy in loads:
        copy.start()
    c_loads = [
        pltpu.make_async_copy(
            current_hbm.at[:, :, pl.ds(g * TILE, TILE)], cbuf.at[k * gpp + g], local_sem.at[3]
        )
        for g in range(gpp)
    ]
    for copy in c_loads:
        copy.start()

    barrier = pltpu.get_barrier_semaphore()

    @pl.loop(1, count)
    def _(r):
        peer = lax.rem(flat + r, count)
        pl.semaphore_signal(
            barrier, inc=1, device_id=(lax.div(peer, bonds), lax.rem(peer, bonds)), device_id_type=MESH
        )

    pl.semaphore_wait(barrier, count - 1)

    def remote(src, dst, ss, rs, kk, dest):
        return pltpu.make_async_remote_copy(
            src_ref=src, dst_ref=dst, send_sem=ss, recv_sem=rs, device_id=(kk, dest), device_id_type=MESH
        )

    def act(copy, drain):
        if drain:
            copy.wait_send()
        else:
            copy.start()


    def e_copy(blk, h, dest):
        ref = ebuf.at[blk, h]
        return remote(ref, ref, e_send, e_recv.at[blk, h], k, dest)

    def spread(blk, h, drain):
        @pl.when(y > 0)
        def _():
            act(e_copy(blk, h, slot(z, y - 1, c)), drain)

        @pl.when(y < ny - 1)
        def _():
            act(e_copy(blk, h, slot(z, y + 1, c)), drain)

        act(e_copy(blk, h, sib), drain)

    def column(i, drain=False):
        for h in range(PARTS):
            if i == 0:
                @pl.when(z > 0)
                def _():
                    act(e_copy(me, h, slot(z - 1, y, c)), drain)

                @pl.when(z < nz - 1)
                def _():
                    act(e_copy(me, h, slot(z + 1, y, c)), drain)

                spread(me, h, drain)
                continue
            for sign in (1, -1):
                zz = z - sign * i
                onward = z + sign

                @pl.when(both(zz >= 0, zz < nz))
                def _():
                    blk = slot(zz, y, c)
                    if not drain:
                        e_copy(blk, h, me).wait_recv()

                    @pl.when(both(onward >= 0, onward < nz))
                    def _():
                        act(e_copy(blk, h, slot(onward, y, c)), drain)

                    spread(blk, h, drain)

    def turn(j):
        least = jnp.minimum(z, nz - 1 - z)
        near = (j + 1) // 2
        inner = z - near if j % 2 else z + near
        far = j - least
        outer = jnp.where(z <= nz - 1 - z, z + far, z - far)
        return jnp.where(j <= 2 * least, inner, outer)

    def across(j, drain=False):
        zz = turn(j)
        for h in range(PARTS):
            for u in range(1, ny):
                for sign in (1, -1):
                    yy = y - sign * u
                    onward = y + sign

                    @pl.when(both(yy >= 0, yy < ny))
                    def _():
                        blk = slot(zz, yy, c)
                        if not drain:
                            e_copy(blk, h, me).wait_recv()

                        @pl.when(both(onward >= 0, onward < ny))
                        def _():
                            act(e_copy(blk, h, slot(z, onward, c)), drain)

                        act(e_copy(blk, h, sib), drain)

    def sibling(j):
        zz = turn(j)
        for h in range(PARTS):
            for yy in range(ny):
                e_copy(slot(zz, yy, 1 - c), h, me).wait_recv()


    def a_copy(h, zz, cc, dest):
        ref = abuf.at[h, zz, :, cc]
        return remote(ref, ref, a_send, a_recv.at[h, zz, cc], k, dest)

    def a_own(sign, drain=False):
        @pl.loop(0, nch)
        def _(h):
            act(a_copy(h, z, c, slot(z + sign, y, c)), drain)

    def a_edges(i, drain=False):
        @pl.when(both(z == i, z < nz - 1))
        def _():
            a_own(1, drain)

        @pl.when(both(nz - 1 - z == i, z > 0))
        def _():
            a_own(-1, drain)

    def a_sibling(drain=False):
        @pl.loop(0, nch)
        def _(h):
            act(a_copy(h, z, c, sib), drain)

    def a_pass(h, i, drain=False):
        for sign in (1, -1):
            zz = z - sign * i
            onward = z + sign

            @pl.when(both(zz >= 0, zz < nz, onward >= 0, onward < nz))
            def _():
                if not drain:
                    a_copy(h, zz, c, me).wait_recv()
                act(a_copy(h, zz, c, slot(onward, y, c)), drain)
                act(a_copy(h, zz, c, sib), drain)

    def a_last(h, i, drain=False):
        for sign in (1, -1):
            zz = z - sign * i
            onward = z + sign

            @pl.when(both(zz >= 0, zz < nz, jnp.logical_or(onward < 0, onward >= nz)))
            def _():
                if not drain:
                    a_copy(h, zz, c, me).wait_recv()
                act(a_copy(h, zz, c, sib), drain)

    def a_ready(h):
        for zz in range(nz):
            a_copy(h, zz, 1 - c, me).wait_recv()


    def c_copy(zz, peer):
        ref = cbuf.at[pl.ds(zz * tpp, tpp)]
        return remote(ref, ref, c_send, c_recv, peer, me)

    def owner_of(zz):
        return lax.div(zz * tpp, gpp)

    def share(drain=False):
        zz = turn(nz - 1)

        @pl.when(owner_of(zz) == k)
        def _():
            for other in range(1, states):
                act(c_copy(zz, lax.rem(k + other, states)), drain)


    def p_copy(g, part_of, peer):
        return remote(
            psend.at[g, part_of], precv.at[k, lax.rem(g, gpp), part_of],
            p_send, p_recv.at[k, lax.div(g, tpp)], peer, me,
        )

    def span(zz):
        return pl.ds(pl.multiple_of(zz * piece, 128), piece)

    def my_copy(zz, yy):
        return remote(
            mown.at[zz, yy], mbuf.at[k, y, :, span(zz)], my_send, my_recv.at[zz, y], k, slot(z, yy, c)
        )

    def mx_copy(zz, yy, peer):
        ref = mbuf.at[k, yy, :, span(zz)]
        return remote(ref, ref, mx_send, mx_recv.at[k], peer, me)

    def flat_of(kk, at):
        return precv[kk, at].reshape(pairs * w, TILE).astype(jnp.float32)

    def halves(whole):
        return whole.astype(jnp.bfloat16).reshape(PARTS, pairs * w // PARTS, TILE)

    def tally(kk, g, whole):
        here = cbuf[g].reshape(pairs * w, TILE).astype(jnp.float32)
        line[kk] += jnp.sum((whole * here).reshape(pairs * w // 8, 8, TILE), axis=0)

    def p_wait(j, use):
        zz = turn(j)

        @pl.when(owner_of(zz) == k)
        def _():
            first = lax.rem(zz * tpp, gpp)
            for other in range(1, states):
                peer = lax.rem(k + other, states)
                ref = precv.at[peer, pl.ds(first, tpp)]
                remote(ref, ref, p_send, p_recv.at[peer, zz], peer, me).wait_recv()
                if use:
                    @pl.loop(0, tpp)
                    def _(r):
                        tally(peer, zz * tpp + r, flat_of(peer, first + r))

    def project(j):
        zz = turn(j)

        if j == nz - 1:
            @pl.when(owner_of(zz) != k)
            def _():
                c_copy(zz, k).wait_recv()

        @pl.loop(0, tpp)
        def _(r):
            g = zz * tpp + r
            left = ebuf[pl.ds(g * per_group, per_group)].reshape(TILE, width)
            prod = lax.dot_general(
                stored[...], left, (((1,), (1,)), ((), ())), preferred_element_type=jnp.float32
            )
            for q in range(cpt):
                yy = r * cpt + q
                moved = jnp.concatenate(
                    [
                        prod[(pairs + s) * w : (pairs + s + 1) * w, q * cell : (q + 1) * cell]
                        for s in range(phys)
                    ],
                    axis=1,
                ).astype(jnp.bfloat16)

                @pl.when(yy == y)
                def _():
                    mbuf[k, y, :, span(zz)] = moved
                    for other in range(1, states):
                        mx_copy(zz, y, lax.rem(k + other, states)).start()

                @pl.when(yy != y)
                def _():
                    mown[zz, yy] = moved
                    if j >= nz - 2:
                        my_copy(zz, yy).start()

            whole = prod[: pairs * w]
            owner = lax.div(g, gpp)

            @pl.when(jnp.logical_or(owner == k, j == nz - 1))
            def _():
                tally(k, g, whole)

            @pl.when(owner == k)
            def _():
                precv[k, lax.rem(g, gpp)] = halves(whole)

            @pl.when(owner != k)
            def _():
                psend[g] = halves(whole)

    def hand_over(j, n, drain=False):
        zz = turn(j)
        g = zz * tpp + n // PARTS
        for other in range(1, states):
            peer = lax.rem(k + other, states)

            @pl.when(lax.div(g, gpp) == peer)
            def _():
                act(p_copy(g, n % PARTS, peer), drain)

    def forward(j, drain=False):
        zz = turn(j)
        for u in range(1, ny):
            yy = lax.rem(y + u, ny)
            if not drain:
                ref = mbuf.at[k, yy, :, span(zz)]
                remote(ref, ref, my_send, my_recv.at[zz, yy], k, me).wait_recv()
            for other in range(1, states):
                act(mx_copy(zz, yy, lax.rem(k + other, states)), drain)


    def t_copy(zc, yy):
        return remote(
            part.at[zc, yy], prt.at[zc, y], t_send, t_recv.at[zc, y], k, slot(z, yy, c)
        )

    def grow(h):
        total = jnp.dot(
            mbuf[...].reshape(ecols, nz * piece),
            abuf[h].reshape(nz * piece, fch),
            preferred_element_type=jnp.float32,
        )
        for q in range(bpc):
            if direct:
                zc, yy = h, q
            else:
                fb = h * bpc + q
                zc = lax.div(fb, ny * nc) * nc + lax.rem(fb, nc)
                yy = lax.rem(lax.div(fb, nc), ny)
            block = total[:, q * w : (q + 1) * w]

            @pl.when(yy == y)
            def _():
                acc[zc] = block

            @pl.when(yy != y)
            def _():
                part[zc, yy] = block.astype(jnp.bfloat16)
                t_copy(zc, yy).start()

    def target(kk, zc):
        return slot(kk * (nz // states) + lax.div(zc, nc), y, lax.rem(zc, nc))

    def place(src):
        if direct:
            return next_hbm.at[:, pl.ds(pl.multiple_of(src * w, 128), w)]
        return next_hbm.at[src]


    def n_copy(kk, zc, yy):
        return remote(
            nbuf.at[kk, zc, yy], place(slot(z, yy, c)), n_send, n_recv, k, target(kk, zc)
        )

    def n_local(kk, zc, yy):
        return pltpu.make_async_copy(nbuf.at[kk, zc, yy], place(slot(z, yy, c)), out_sem.at[1])

    def deliver(kk, zc, drain=False):
        stays = target(kk, zc) == me
        for yy in range(ny):
            @pl.when(stays)
            def _():
                if drain:
                    n_local(kk, zc, yy).wait()
                else:
                    n_local(kk, zc, yy).start()

            @pl.when(jnp.logical_not(stays))
            def _():
                act(n_copy(kk, zc, yy), drain)

    def r_copy(kk, zc):
        return remote(nsend.at[kk, zc], nbuf.at[k, zc], r_send, r_recv.at[k, zc], kk, me)

    def finish(zc):
        total = acc[zc]
        for u in range(1, ny):
            yy = lax.rem(y + u, ny)
            ref = prt.at[zc, yy]
            remote(ref, ref, t_send, t_recv.at[zc, yy], k, me).wait_recv()
            total = total + ref[...].astype(jnp.float32)
        for kk in range(states):
            blocks = [
                total[(kk * ny + yy) * w : (kk * ny + yy + 1) * w].T.astype(jnp.bfloat16)
                for yy in range(ny)
            ]

            @pl.when(kk == k)
            def _():
                for yy in range(ny):
                    nbuf[k, zc, yy] = blocks[yy]
                deliver(k, zc)

            @pl.when(kk != k)
            def _():
                for yy in range(ny):
                    nsend[kk, zc, yy] = blocks[yy]
                r_copy(kk, zc).start()

    def pass_on(zc):
        for other in range(1, states):
            kk = lax.rem(k + other, states)
            ref = nbuf.at[kk, zc]
            remote(ref, ref, r_send, r_recv.at[kk, zc], k, me).wait_recv()
            deliver(kk, zc)


    def i_near(u):
        there = lax.rem(lax.rem(me, near) + u, near)
        ref = iplane.at[lax.rem(me, near)]
        return remote(ref, ref, i_send.at[0], i_recv.at[0], k, z * near + there)

    def i_far(u):
        ref = iline.at[z]
        return remote(ref, ref, i_send.at[1], i_recv.at[1], k, slot(lax.rem(z + u, nz), y, c))

    def i_peer(u):
        ref = istate.at[k]
        return remote(ref, ref, i_send.at[2], i_recv.at[2], lax.rem(k + u, states), me)

    stages = ((i_near, near, iplane), (i_far, nz, iline), (i_peer, states, istate))

    def start(n):
        send, number, _ = stages[n]
        for u in range(1, number):
            send(u).start()

    def gathered(n):
        _, number, buf = stages[n]
        rest = buf.at[pl.ds(0, number - 1)]
        remote(rest, rest, i_send.at[n], i_recv.at[n], k, me).wait_recv()

    def overlap(n):
        if n == 0:
            for kk in range(states):
                short = jnp.sum(line[kk], axis=0, keepdims=True)
                total = short[:, :128]
                for at in range(128, TILE, 128):
                    total = total + short[:, at : at + 128]
                iplane[lax.rem(me, near), kk : kk + 1] = total
        elif n == 1:
            gathered(0)
            iline[z] = jnp.sum(iplane[...], axis=0)
        else:
            gathered(1)
            istate[k] = jnp.sum(iline[...], axis=0)
        start(n)

    pen_copies = [
        pltpu.make_async_copy(pen.at[g], pen_hbm.at[:, :, pl.ds(g * TILE, TILE)], out_sem.at[0])
        for g in range(gpp)
    ]

    def penalize():
        gathered(2)
        p_wait(nz - 1, False)
        scale = 1.0 / (phys * width)
        factors = [weight_ref[kk] * (jnp.sum(istate[:, kk]) * scale) for kk in range(states)]
        for g in range(gpp):
            value = cbuf[k * gpp + g].reshape(pairs * w, TILE).astype(jnp.float32)
            for kk in range(states):
                value = value + factors[kk] * flat_of(kk, g)
            pen[g] = value.reshape(pairs, w, TILE)
            pen_copies[g].start()

    line[...] = jnp.zeros_like(line)
    e_load.wait()
    for i in range(nz + 1):
        if i < nz:
            column(i)
            if i == 0:
                for copy in a_loads:
                    copy.wait()
                a_sibling()
            a_edges(i)
            if i == 0:
                for copy in c_loads:
                    copy.wait()
                share()
        if i == nz - 1:
            for j in range(nz - 2):
                for u in range(1, ny):
                    my_copy(turn(j), lax.rem(y + u, ny)).start()
        if i >= 1:
            across(i - 1)
            sibling(i - 1)
            if i == 1:
                for copy in loads:
                    copy.wait()
            project(i - 1)
            if i < nz:
                for n in range(slices - (i == nz - 1)):
                    hand_over(i - 1, n)
        if i == nz - 1:
            @pl.loop(0, nch)
            def _(h):
                a_pass(h, 1)

    for i in range(2, nz):
        @pl.loop(0, nch)
        def _(h):
            a_pass(h, i)

    for j in range(nz):
        forward(j)
        if 1 <= j < nz - 1:
            @pl.loop(0, nch)
            def _(h):
                a_last(h, j)
    for i in range(nz):
        column(i, drain=True)
        across(i, drain=True)
    a_last(0, nz - 1)
    for other in range(1, states):
        peer = lax.rem(k + other, states)
        ref = mbuf.at[peer]
        remote(ref, ref, mx_send, mx_recv.at[peer], peer, me).wait_recv()

    @pl.loop(0, nch)
    def _(h):
        a_ready(h)
        grow(h)

        @pl.when(h == 0)
        def _():
            hand_over(nz - 2, slices - 1)

        for n in range(slices):
            @pl.when(h == n * nch // slices)
            def _():
                hand_over(nz - 1, n)

        @pl.when(h < nch - 1)
        def _():
            a_last(h + 1, nz - 1)

        @pl.when(h == max(nch - 2, 0))
        def _():
            for j in range(nz - 1):
                p_wait(j, True)
            overlap(0)

        if direct:
            @pl.when(h > 1)
            def _():
                finish(h - 2)

        @pl.when(h == nch - 1)
        def _():
            overlap(1)

    for i in range(nz):
        a_edges(i, drain=True)
    a_sibling(drain=True)

    @pl.loop(0, nch)
    def _(h):
        for i in range(1, nz):
            a_pass(h, i, drain=True)
            a_last(h, i, drain=True)

    if direct:
        for h in range(nch - 2, nch):
            finish(h)
            if h < nch - 1:
                overlap(2)
                pass_on(h - nch + 2)
        for h in range(1, nch):
            pass_on(h)
    else:
        @pl.loop(0, mine)
        def _(zc):
            finish(zc)

        overlap(2)

        @pl.loop(0, mine)
        def _(zc):
            pass_on(zc)

    penalize()

    for i in range(nz):
        forward(i, drain=True)
        for n in range(slices):
            hand_over(i, n, drain=True)

    @pl.loop(0, nz)
    def _(zz):
        for u in range(1, ny):
            my_copy(zz, lax.rem(y + u, ny)).wait_send()
        for other in range(1, states):
            mx_copy(zz, y, lax.rem(k + other, states)).wait_send()

    share(drain=True)
    for send, number, _ in stages:
        for u in range(1, number):
            send(u).wait_send()

    @pl.loop(0, mine)
    def _(zc):
        for u in range(1, ny):
            t_copy(zc, lax.rem(y + u, ny)).wait_send()
        for kk in range(states):
            @pl.when(kk != k)
            def _():
                r_copy(kk, zc).wait_send()

            deliver(kk, zc, drain=True)

    for copy in pen_copies:
        copy.wait()
    if direct:
        rest = next_hbm.at[:, pl.ds(0, (bonds - ny) * w)]
    else:
        rest = next_hbm.at[pl.ds(0, bonds - ny)]
    remote(rest, rest, n_send, n_recv, k, me).wait_recv()


def shards(states, bonds, intersect_left, stored_block, stored_site, current_site, current_block, penalty_weight):
    rows, width = intersect_left.shape[1:]
    pairs, w = stored_block.shape[1:3]
    phys = stored_site.shape[1]
    fwidth = current_site.shape[2]
    groups = width // TILE
    gpp = groups // states
    ny = 1
    while 4 * ny * ny <= bonds // CORES:
        ny *= 2
    nz = bonds // (CORES * ny)
    direct = w % 128 == 0
    fch = ny * w if direct else max(w, 128)
    nch, mine = fwidth // fch, fwidth // w // ny
    cell = CORES * rows
    piece = phys * cell
    bf, f32 = jnp.bfloat16, jnp.float32
    anywhere = pl.BlockSpec(memory_space=pl.ANY)
    dma = pltpu.SemaphoreType.DMA
    penalized, grown = pl.pallas_call(
        functools.partial(kernel, states, bonds, ny, fch),
        out_shape=(
            jax.ShapeDtypeStruct(current_block.shape, f32),
            jax.ShapeDtypeStruct((w, bonds * w) if direct else (bonds, w, w), bf),
        ),
        in_specs=[anywhere] * 5 + [pl.BlockSpec(memory_space=pltpu.SMEM)],
        out_specs=(anywhere, anywhere),
        scratch_shapes=[
            pltpu.VMEM((bonds, PARTS, rows // PARTS, width), bf),
            pltpu.VMEM((nch, nz, phys, CORES, rows, fch), bf),
            pltpu.VMEM(((pairs + phys) * w, width), bf),
            pltpu.VMEM((groups, pairs, w, TILE), bf),
            pltpu.VMEM((groups, PARTS, pairs * w // PARTS, TILE), bf),
            pltpu.VMEM((states, gpp, PARTS, pairs * w // PARTS, TILE), bf),
            pltpu.VMEM((nz, ny, w, piece), bf),
            pltpu.VMEM((states, ny, w, nz * piece), bf),
            pltpu.VMEM((mine, states * ny * w, w), f32),
            pltpu.VMEM((mine, ny, states * ny * w, w), bf),
            pltpu.VMEM((mine, ny, states * ny * w, w), bf),
            pltpu.VMEM((states, mine, ny, w, w), bf),
            pltpu.VMEM((states, mine, ny, w, w), bf),
            pltpu.VMEM((gpp, pairs, w, TILE), f32),
            pltpu.VMEM((CORES * ny, states, 128), f32),
            pltpu.VMEM((nz, states, 128), f32),
            pltpu.VMEM((states, states, 128), f32),
            pltpu.VMEM((states, 8, TILE), f32),
            dma((4,)), dma((2,)),
            dma, dma((bonds, PARTS)),
            dma, dma((nch, nz, CORES)),
            dma, dma((states, nz)),
            dma, dma((nz, ny)),
            dma, dma((states,)),
            dma, dma,
            dma((3,)), dma((3,)),
            dma, dma((mine, ny)),
            dma, dma((states, mine)),
            dma, dma,
        ],
        compiler_params=pltpu.CompilerParams(
            collective_id=0, has_side_effects=True, vmem_limit_bytes=60 * 1024 * 1024
        ),
    )(
        intersect_left.reshape(PARTS, rows // PARTS, width), stored_block[0], stored_site[0],
        current_site.reshape(rows, phys * fwidth), current_block, penalty_weight,
    )
    if direct:
        return penalized, grown[None]
    return penalized, grown.transpose(1, 0, 2).reshape(1, w, bonds * w)


def solution(mesh):
    placed = (
        P("state", "bond", None),
        P("state", None, "bond", None),
        P("state", None, "bond", None),
        P("bond", None, "state"),
        P(None, "bond", "state"),
        P(),
    )
    return jax.shard_map(
        functools.partial(shards, mesh.shape["state"], mesh.shape["bond"]),
        mesh=mesh,
        in_specs=placed,
        out_specs=(P(None, "bond", "state"), P("state", "bond", None)),
        check_vma=False,
    )
```

time: 134 us -> 106 us (0.79)
  the two profiles are of different devices: /device:TPU:27 before, /device:TPU:25 now
where the time goes in v1:
time: 106 us; the launch traced here: 105 us
  Pallas kernels  98.8 us (93%)
  local copies, waits for them, and re-layouts  5.97 us (6%)
    pallas_call x1, Pallas kernels, shards(): pl.pallas_call(functools.partial(kernel, states, bonds, ny, fch), out_sha...  98.8 us
    unnamed x5, local copies, waits for them, and re-layouts  5.97 us

profile of v1, /device:TPU:25, one launch (start us, length us, event | category | flops | bytes accessed | tf_op | source)
XLA Modules:
  0.0 105.4 jit_solution(1322807764335185615)
XLA Ops:
  0.6 2.0 %copy.8 = bf16[16,8,2,1024]{3,1,2,0:T(8,128)(2,1)} copy(bf16[16,8,2,1024]{3,2,1,0:T(2,128)(2,1)} %bitcast.9) | data formatting | bytes 1048576
  2.6 98.8 %shard_map.77 = (f32[4,128,1024]{2,1,0:T(8,128)}, bf16[128,2048]{1,0:T(8,128)(2,1)}) custom-call(bf16[2,64,2048]{2,1,0:T(8,128)(2,1)} %bitcast.11, bf16[4,128,2048]{2,1,0:T(8,128)(2,1)} %bitcast.6, bf16[2,128,2048]{2,1,0:T(8,128)(2,1)} %bitcast.8, bf16[128,2048]{1,0:T(8,128)(2,1)} %bitcast.7, bf16[4,128,1024]{2,1,0:T(8,128)(2,1)} %current_hbm.1, f32[2]{0:T(128)} %weight_ref.1), custom_call_target="tpu_custom_call" | custom-call | tf_op jit(solution)/shard_map/pallas_call | solution.py:715
  101.4 0.0 copy-start
  101.4 3.2 %copy.11 = f32[4,128,1024]{2,1,0:T(8,128)} copy(f32[4,128,1024]{2,1,0:T(8,128)} %get-tuple-element.8) | data formatting | bytes 4194304
  104.6 0.0 copy-done
  104.6 0.8 copy.12
Async XLA Ops:
  101.4 3.2 %copy-start = (bf16[128,2048]{1,0:T(8,128)(2,1)S(1)}, bf16[128,2048]{1,0:T(8,128)(2,1)}, u32[]{:S(2)}) copy-start(bf16[128,2048]{1,0:T(8,128)(2,1)} %get-tuple-element.5) | copy-start | bytes 1572868

commit v2 on v1

--- a/solution.py
+++ b/solution.py
@@ -21,7 +21,7 @@
     states, bonds, rows_y, fch,
     env_hbm, block_hbm, site_hbm, grow_hbm, current_hbm, weight_ref,
     pen_hbm, next_hbm,
-    ebuf, abuf, stored, cbuf, psend, precv, mown, mbuf, acc, part, prt, nsend, nbuf, pen, iplane, iline, istate, line,
+    ebuf, raw, abuf, stored, cbuf, psend, precv, mown, mbuf, acc, part, prt, nsend, nbuf, pen, iplane, iline, istate, line,
     local_sem, out_sem, e_send, e_recv, a_send, a_recv, p_send, p_recv, my_send, my_recv, mx_send, mx_recv,
     c_send, c_recv, i_send, i_recv, t_send, t_recv, r_send, r_recv, n_send, n_recv,
 ):
@@ -31,7 +31,7 @@
     rows = hr * PARTS
     pairs, w = block_hbm.shape[:2]
     phys = site_hbm.shape[0]
-    fwidth = grow_hbm.shape[1] // phys
+    fwidth = grow_hbm.shape[2]
     nch = fwidth // fch
     bpc = fch // w
     fbs = fwidth // w
@@ -42,7 +42,6 @@
     cpt = TILE // cell
     groups = width // TILE
     gpp = groups // states
-    count = states * bonds
     ecols = states * ny * w
     direct = w % 128 == 0
     piece = phys * cell
@@ -52,7 +51,6 @@
     c = lax.rem(me, nc)
     y = lax.rem(lax.div(me, nc), ny)
     z = lax.div(me, nc * ny)
-    flat = k * bonds + me
     near = ny * nc
     slices = PARTS * tpp
 
@@ -68,20 +66,8 @@
 
     e_load = pltpu.make_async_copy(env_hbm, ebuf.at[me], local_sem.at[0])
     e_load.start()
-    a_loads = []
-    for h in range(nch):
-        for s in range(phys):
-            for q in range(bpc if direct else 1):
-                size = w if direct else fch
-                a_loads.append(
-                    pltpu.make_async_copy(
-                        grow_hbm.at[:, pl.ds(s * fwidth + column_of(h, q) * w, size)],
-                        abuf.at[h, z, s, c, :, pl.ds(q * w, size)],
-                        local_sem.at[1],
-                    )
-                )
-    for copy in a_loads:
-        copy.start()
+    a_load = pltpu.make_async_copy(grow_hbm, raw, local_sem.at[1])
+    a_load.start()
     loads = []
     for q in range(pairs):
         loads.append(pltpu.make_async_copy(block_hbm.at[q], stored.at[pl.ds(q * w, w)], local_sem.at[2]))
@@ -102,14 +88,23 @@
 
     barrier = pltpu.get_barrier_semaphore()
 
-    @pl.loop(1, count)
-    def _(r):
-        peer = lax.rem(flat + r, count)
-        pl.semaphore_signal(
-            barrier, inc=1, device_id=(lax.div(peer, bonds), lax.rem(peer, bonds)), device_id_type=MESH
-        )
-
-    pl.semaphore_wait(barrier, count - 1)
+    def greet(kk, dest):
+        pl.semaphore_signal(barrier, inc=1, device_id=(kk, dest), device_id_type=MESH)
+
+    @pl.when(z > 0)
+    def _():
+        greet(k, slot(z - 1, y, c))
+
+    @pl.when(z < nz - 1)
+    def _():
+        greet(k, slot(z + 1, y, c))
+
+    for other in range(1, near):
+        greet(k, z * near + lax.rem(lax.rem(me, near) + other, near))
+    for other in range(1, states):
+        greet(lax.rem(k + other, states), me)
+    ends = jnp.where(z > 0, 1, 0) + jnp.where(z < nz - 1, 1, 0)
+    pl.semaphore_wait(barrier, near + states - 2 + ends)
 
     def remote(src, dst, ss, rs, kk, dest):
         return pltpu.make_async_remote_copy(
@@ -201,6 +196,14 @@
             for yy in range(ny):
                 e_copy(slot(zz, yy, 1 - c), h, me).wait_recv()
 
+
+    def unpack():
+        for s in range(phys):
+            plain = raw[:, s, :]
+            for h in range(nch):
+                for q in range(bpc):
+                    at = column_of(h, q) * w
+                    abuf[h, z, s, c, :, q * w : (q + 1) * w] = plain[:, at : at + w]
 
     def a_copy(h, zz, cc, dest):
         ref = abuf.at[h, zz, :, cc]
@@ -545,8 +548,8 @@
         if i < nz:
             column(i)
             if i == 0:
-                for copy in a_loads:
-                    copy.wait()
+                a_load.wait()
+                unpack()
                 a_sibling()
             a_edges(i)
             if i == 0:
@@ -601,8 +604,8 @@
         def _():
             hand_over(nz - 2, slices - 1)
 
-        for n in range(slices):
-            @pl.when(h == n * nch // slices)
+        for n in range(slices - 1):
+            @pl.when(h == min(n + 1, nch - 1))
             def _():
                 hand_over(nz - 1, n)
 
@@ -621,10 +624,32 @@
             def _():
                 finish(h - 2)
 
-        @pl.when(h == nch - 1)
-        def _():
-            overlap(1)
-
+    if direct:
+        pass_on(0)
+        overlap(1)
+        finish(nch - 2)
+        for h in range(1, nch - 2):
+            pass_on(h)
+        finish(nch - 1)
+        hand_over(nz - 1, slices - 1)
+        overlap(2)
+        for h in range(max(nch - 2, 1), nch):
+            pass_on(h)
+    else:
+        hand_over(nz - 1, slices - 1)
+        overlap(1)
+
+        @pl.loop(0, mine)
+        def _(zc):
+            finish(zc)
+
+        overlap(2)
+
+        @pl.loop(0, mine)
+        def _(zc):
+            pass_on(zc)
+
+    penalize()
     for i in range(nz):
         a_edges(i, drain=True)
     a_sibling(drain=True)
@@ -634,27 +659,6 @@
         for i in range(1, nz):
             a_pass(h, i, drain=True)
             a_last(h, i, drain=True)
-
-    if direct:
-        for h in range(nch - 2, nch):
-            finish(h)
-            if h < nch - 1:
-                overlap(2)
-                pass_on(h - nch + 2)
-        for h in range(1, nch):
-            pass_on(h)
-    else:
-        @pl.loop(0, mine)
-        def _(zc):
-            finish(zc)
-
-        overlap(2)
-
-        @pl.loop(0, mine)
-        def _(zc):
-            pass_on(zc)
-
-    penalize()
 
     for i in range(nz):
         forward(i, drain=True)
@@ -722,6 +726,7 @@
         out_specs=(anywhere, anywhere),
         scratch_shapes=[
             pltpu.VMEM((bonds, PARTS, rows // PARTS, width), bf),
+            pltpu.VMEM((rows, phys, fwidth), bf),
             pltpu.VMEM((nch, nz, phys, CORES, rows, fch), bf),
             pltpu.VMEM(((pairs + phys) * w, width), bf),
             pltpu.VMEM((groups, pairs, w, TILE), bf),
@@ -756,7 +761,7 @@
         ),
     )(
         intersect_left.reshape(PARTS, rows // PARTS, width), stored_block[0], stored_site[0],
-        current_site.reshape(rows, phys * fwidth), current_block, penalty_weight,
+        current_site, current_block, penalty_weight,
     )
     if direct:
         return penalized, grown[None]

time: 106 us -> 101 us (0.953)
  Pallas kernels: 98.8 us -> 95.3 us
  local copies, waits for them, and re-layouts: 5.97 us -> 4.01 us
    pallas_call x1, Pallas kernels: 98.8 us -> 95.3 us  [shards(): pl.pallas_call(functools.partial(kernel, states, bonds, ny, fch), out_sha...]
    unnamed x5 -> x4, local copies, waits for them, and re-layouts: 5.97 us -> 4.01 us
where the time goes in v2:
time: 101 us; the launch traced here: 100 us
  Pallas kernels  95.3 us (94%)
  local copies, waits for them, and re-layouts  4.01 us (4%)
    pallas_call x1, Pallas kernels, shards(): pl.pallas_call(functools.partial(kernel, states, bonds, ny, fch), out_sha...  95.3 us
    unnamed x4, local copies, waits for them, and re-layouts  4.01 us

profile of v2, /device:TPU:25, one launch (start us, length us, event | category | flops | bytes accessed | tf_op | source)
XLA Modules:
  0.0 100.0 jit_solution(13112161936344304440)
XLA Ops:
  0.6 95.3 %shard_map.77 = (f32[4,128,1024]{2,1,0:T(8,128)}, bf16[128,2048]{1,0:T(8,128)(2,1)}) custom-call(bf16[2,64,2048]{2,1,0:T(8,128)(2,1)} %bitcast.7, bf16[4,128,2048]{2,1,0:T(8,128)(2,1)} %bitcast.4, bf16[2,128,2048]{2,1,0:T(8,128)(2,1)} %bitcast.5, bf16[128,2,1024]{2,1,0:T(2,128)(2,1)} %grow_hbm.1, bf16[4,128,1024]{2,1,0:T(8,128)(2,1)} %current_hbm.1, f32[2]{0:T(128)} %weight_ref.1), custom_call_target="tpu_custom_call" | custom-call | tf_op jit(solution)/shard_map/pallas_call | solution.py:719
  96.0 0.0 copy-start
  96.0 3.2 %copy.10 = f32[4,128,1024]{2,1,0:T(8,128)} copy(f32[4,128,1024]{2,1,0:T(8,128)} %get-tuple-element.8) | data formatting | bytes 4194304
  99.2 0.0 copy-done
  99.2 0.8 copy.11
Async XLA Ops:
  96.0 3.2 %copy-start = (bf16[128,2048]{1,0:T(8,128)(2,1)S(1)}, bf16[128,2048]{1,0:T(8,128)(2,1)}, u32[]{:S(2)}) copy-start(bf16[128,2048]{1,0:T(8,128)(2,1)} %get-tuple-element.5) | copy-start | bytes 1572868

commit v3 on v2

--- a/solution.py
+++ b/solution.py
@@ -20,9 +20,9 @@
 def kernel(
     states, bonds, rows_y, fch,
     env_hbm, block_hbm, site_hbm, grow_hbm, current_hbm, weight_ref,
-    pen_hbm, next_hbm,
-    ebuf, raw, abuf, stored, cbuf, psend, precv, mown, mbuf, acc, part, prt, nsend, nbuf, pen, iplane, iline, istate, line,
-    local_sem, out_sem, e_send, e_recv, a_send, a_recv, p_send, p_recv, my_send, my_recv, mx_send, mx_recv,
+    pen_ref, next_ref,
+    ebuf, raw, abuf, stored, cbuf, psend, precv, mown, mbuf, acc, part, prt, nsend, nbuf, iplane, iline, istate, line,
+    local_sem, e_send, e_recv, a_send, a_recv, p_send, p_recv, my_send, my_recv, mx_send, mx_recv,
     c_send, c_recv, i_send, i_recv, t_send, t_recv, r_send, r_recv, n_send, n_recv,
 ):
     nc, ny = CORES, rows_y
@@ -422,8 +422,8 @@
 
     def place(src):
         if direct:
-            return next_hbm.at[:, pl.ds(pl.multiple_of(src * w, 128), w)]
-        return next_hbm.at[src]
+            return next_ref.at[:, pl.ds(pl.multiple_of(src * w, 128), w)]
+        return next_ref.at[src]
 
 
     def n_copy(kk, zc, yy):
@@ -431,18 +431,13 @@
             nbuf.at[kk, zc, yy], place(slot(z, yy, c)), n_send, n_recv, k, target(kk, zc)
         )
 
-    def n_local(kk, zc, yy):
-        return pltpu.make_async_copy(nbuf.at[kk, zc, yy], place(slot(z, yy, c)), out_sem.at[1])
-
     def deliver(kk, zc, drain=False):
         stays = target(kk, zc) == me
         for yy in range(ny):
-            @pl.when(stays)
-            def _():
-                if drain:
-                    n_local(kk, zc, yy).wait()
-                else:
-                    n_local(kk, zc, yy).start()
+            if not drain:
+                @pl.when(stays)
+                def _():
+                    place(slot(z, yy, c))[...] = nbuf[kk, zc, yy]
 
             @pl.when(jnp.logical_not(stays))
             def _():
@@ -525,11 +520,6 @@
             istate[k] = jnp.sum(iline[...], axis=0)
         start(n)
 
-    pen_copies = [
-        pltpu.make_async_copy(pen.at[g], pen_hbm.at[:, :, pl.ds(g * TILE, TILE)], out_sem.at[0])
-        for g in range(gpp)
-    ]
-
     def penalize():
         gathered(2)
         p_wait(nz - 1, False)
@@ -539,8 +529,7 @@
             value = cbuf[k * gpp + g].reshape(pairs * w, TILE).astype(jnp.float32)
             for kk in range(states):
                 value = value + factors[kk] * flat_of(kk, g)
-            pen[g] = value.reshape(pairs, w, TILE)
-            pen_copies[g].start()
+            pen_ref[:, :, g * TILE : (g + 1) * TILE] = value.reshape(pairs, w, TILE)
 
     line[...] = jnp.zeros_like(line)
     e_load.wait()
@@ -688,12 +677,10 @@
 
             deliver(kk, zc, drain=True)
 
-    for copy in pen_copies:
-        copy.wait()
     if direct:
-        rest = next_hbm.at[:, pl.ds(0, (bonds - ny) * w)]
+        rest = next_ref.at[:, pl.ds(0, (bonds - ny) * w)]
     else:
-        rest = next_hbm.at[pl.ds(0, bonds - ny)]
+        rest = next_ref.at[pl.ds(0, bonds - ny)]
     remote(rest, rest, n_send, n_recv, k, me).wait_recv()
 
 
@@ -714,16 +701,16 @@
     cell = CORES * rows
     piece = phys * cell
     bf, f32 = jnp.bfloat16, jnp.float32
-    anywhere = pl.BlockSpec(memory_space=pl.ANY)
+    anywhere = pl.BlockSpec(memory_space=pltpu.HBM)
     dma = pltpu.SemaphoreType.DMA
     penalized, grown = pl.pallas_call(
         functools.partial(kernel, states, bonds, ny, fch),
         out_shape=(
-            jax.ShapeDtypeStruct(current_block.shape, f32),
-            jax.ShapeDtypeStruct((w, bonds * w) if direct else (bonds, w, w), bf),
+            pltpu.VMEM(current_block.shape, f32),
+            pltpu.VMEM((w, bonds * w) if direct else (bonds, w, w), bf),
         ),
         in_specs=[anywhere] * 5 + [pl.BlockSpec(memory_space=pltpu.SMEM)],
-        out_specs=(anywhere, anywhere),
+        out_specs=(pl.BlockSpec(memory_space=pltpu.VMEM),) * 2,
         scratch_shapes=[
             pltpu.VMEM((bonds, PARTS, rows // PARTS, width), bf),
             pltpu.VMEM((rows, phys, fwidth), bf),
@@ -739,12 +726,11 @@
             pltpu.VMEM((mine, ny, states * ny * w, w), bf),
             pltpu.VMEM((states, mine, ny, w, w), bf),
             pltpu.VMEM((states, mine, ny, w, w), bf),
-            pltpu.VMEM((gpp, pairs, w, TILE), f32),
             pltpu.VMEM((CORES * ny, states, 128), f32),
             pltpu.VMEM((nz, states, 128), f32),
             pltpu.VMEM((states, states, 128), f32),
             pltpu.VMEM((states, 8, TILE), f32),
-            dma((4,)), dma((2,)),
+            dma((4,)),
             dma, dma((bonds, PARTS)),
             dma, dma((nch, nz, CORES)),
             dma, dma((states, nz)),

time: 101 us -> 98.2 us (0.972)
  local copies, waits for them, and re-layouts: 4.01 us -> 2.11 us
    unnamed x4 -> x2, local copies, waits for them, and re-layouts: 4.01 us -> 2.11 us
where the time goes in v3:
time: 98.2 us; the launch traced here: 97.8 us
  Pallas kernels  95.1 us (97%)
  local copies, waits for them, and re-layouts  2.11 us (2%)
    pallas_call x1, Pallas kernels, shards(): pl.pallas_call(functools.partial(kernel, states, bonds, ny, fch), out_sha...  95.1 us
    unnamed x2, local copies, waits for them, and re-layouts  2.11 us

profile of v3, /device:TPU:25, one launch (start us, length us, event | category | flops | bytes accessed | tf_op | source)
XLA Modules:
  0.0 97.8 jit_solution(1863428689516749126)
XLA Ops:
  0.6 95.1 %shard_map.77 = (f32[4,128,1024]{2,1,0:T(8,128)S(1)}, bf16[128,2048]{1,0:T(8,128)(2,1)S(1)}) custom-call(bf16[2,64,2048]{2,1,0:T(8,128)(2,1)} %bitcast.7, bf16[4,128,2048]{2,1,0:T(8,128)(2,1)} %bitcast.5, bf16[2,128,2048]{2,1,0:T(8,128)(2,1)} %bitcast.6, bf16[128,2,1024]{2,1,0:T(2,128)(2,1)} %grow_hbm.1, bf16[4,128,1024]{2,1,0:T(8,128)(2,1)} %current_hbm.1, ...), custom_call_target="tpu_custom_call" | custom-call | tf_op jit(solution)/shard_map/pallas_call | solution.py:706
  95.7 1.3 %copy.10 = f32[4,128,1024]{2,1,0:T(8,128)} copy(f32[4,128,1024]{2,1,0:T(8,128)S(1)} %get-tuple-element.6) | data formatting | bytes 4194304
  97.1 0.8 copy.11

commit v4 on v3

--- a/solution.py
+++ b/solution.py
@@ -59,6 +59,25 @@
 
     sib = slot(z, y, 1 - c)
 
+    def owner_of(zz):
+        return lax.div(zz * tpp, gpp)
+
+    def order(kk, zz):
+        rest = sorted(set(range(nz)) - {zz}, key=lambda other: abs(other - zz))
+        return [zz] + sorted(rest, key=lambda other: other * tpp // gpp == kk)
+
+    def turn_of(kk, j):
+        at = jnp.int32(0)
+        for k_ in range(states):
+            for z_ in range(nz):
+                at = at + jnp.where(both(kk == k_, z == z_), order(k_, z_)[j], 0)
+        return at
+
+    turns = [turn_of(k, j) for j in range(nz)]
+
+    def turn(j):
+        return turns[j]
+
     def column_of(h, q):
         if direct:
             return (h // nc * ny + q) * nc + h % nc
@@ -122,7 +141,7 @@
         ref = ebuf.at[blk, h]
         return remote(ref, ref, e_send, e_recv.at[blk, h], k, dest)
 
-    def spread(blk, h, drain):
+    def spread(blk, h, drain=False):
         @pl.when(y > 0)
         def _():
             act(e_copy(blk, h, slot(z, y - 1, c)), drain)
@@ -131,44 +150,94 @@
         def _():
             act(e_copy(blk, h, slot(z, y + 1, c)), drain)
 
-        act(e_copy(blk, h, sib), drain)
-
-    def column(i, drain=False):
+    def within(zz):
+        return both(zz >= 0, zz < nz)
+
+
+    def late(zz, sign):
+        return both(owner_of(zz) == k, k != (0 if sign > 0 else states - 1))
+
+    def pass_z(zz, h, sign, drain=False):
+        @pl.when(within(z + sign))
+        def _():
+            act(e_copy(slot(zz, y, c), h, slot(z + sign, y, c)), drain)
+
+    def own():
         for h in range(PARTS):
-            if i == 0:
-                @pl.when(z > 0)
-                def _():
-                    act(e_copy(me, h, slot(z - 1, y, c)), drain)
-
-                @pl.when(z < nz - 1)
-                def _():
-                    act(e_copy(me, h, slot(z + 1, y, c)), drain)
-
-                spread(me, h, drain)
-                continue
+            for sign in (1, -1):
+                if h < PARTS - 1:
+                    pass_z(z, h, sign)
+                else:
+                    @pl.when(jnp.logical_not(late(z, sign)))
+                    def _():
+                        pass_z(z, h, sign)
+            spread(me, h)
+            act(e_copy(me, h, sib), False)
+
+    def own_late(sign):
+        @pl.when(late(z, sign))
+        def _():
+            pass_z(z, PARTS - 1, sign)
+
+    def take(zz, h, sign):
+        blk = slot(zz, y, c)
+        e_copy(blk, h, me).wait_recv()
+        pass_z(zz, h, sign)
+        act(e_copy(blk, h, sib), False)
+
+    reach = jnp.maximum(jnp.where(k > 0, z, 0), jnp.where(k < states - 1, nz - 1 - z, 0))
+
+    def natural(i, wanted, parts=range(PARTS)):
+        for h in parts:
             for sign in (1, -1):
                 zz = z - sign * i
-                onward = z + sign
-
-                @pl.when(both(zz >= 0, zz < nz))
+                kept = owner_of(zz) == k
+                mine_now = kept if wanted else jnp.logical_not(kept)
+                if wanted and h == PARTS - 1:
+                    mine_now = both(mine_now, jnp.logical_not(late(zz, sign)))
+
+                @pl.when(both(within(zz), mine_now))
                 def _():
-                    blk = slot(zz, y, c)
-                    if not drain:
-                        e_copy(blk, h, me).wait_recv()
-
-                    @pl.when(both(onward >= 0, onward < nz))
+                    take(zz, h, sign)
+                    if wanted and i < nz - 2:
+                        @pl.when(jnp.logical_or(late(zz, sign), reach <= i))
+                        def _():
+                            spread(slot(zz, y, c), h)
+                    else:
+                        spread(slot(zz, y, c), h)
+
+    def deferred():
+        for i in range(1, nz - 2):
+            for sign in (1, -1):
+                zz = z - sign * i
+
+                @pl.when(both(within(zz), owner_of(zz) == k, reach > i, jnp.logical_not(late(zz, sign))))
+                def _():
+                    for h in range(PARTS):
+                        spread(slot(zz, y, c), h)
+
+    def delayed():
+        for i in range(1, nz):
+            for sign in (1, -1):
+                zz = z - sign * i
+
+                @pl.when(both(within(zz), late(zz, sign)))
+                def _():
+                    take(zz, PARTS - 1, sign)
+                    spread(slot(zz, y, c), PARTS - 1)
+
+    def rows_sent():
+        for h in range(PARTS):
+            for i in range(nz):
+                for sign in (1, -1):
+                    zz = z - sign * i
+
+                    @pl.when(within(zz))
                     def _():
-                        act(e_copy(blk, h, slot(onward, y, c)), drain)
-
-                    spread(blk, h, drain)
-
-    def turn(j):
-        least = jnp.minimum(z, nz - 1 - z)
-        near = (j + 1) // 2
-        inner = z - near if j % 2 else z + near
-        far = j - least
-        outer = jnp.where(z <= nz - 1 - z, z + far, z - far)
-        return jnp.where(j <= 2 * least, inner, outer)
+                        pass_z(zz, h, sign, drain=True)
+                        if i or sign > 0:
+                            spread(slot(zz, y, c), h, drain=True)
+                            act(e_copy(slot(zz, y, c), h, sib), True)
 
     def across(j, drain=False):
         zz = turn(j)
@@ -210,17 +279,27 @@
         return remote(ref, ref, a_send, a_recv.at[h, zz, cc], k, dest)
 
     def a_own(sign, drain=False):
-        @pl.loop(0, nch)
+        @pl.loop(0 if drain else jnp.where(late(z, sign), 1, 0), nch)
         def _(h):
             act(a_copy(h, z, c, slot(z + sign, y, c)), drain)
+
+    def a_first():
+        for sign in (1, -1):
+            @pl.when(both(within(z + sign), late(z, sign)))
+            def _():
+                a_copy(0, z, c, slot(z + sign, y, c)).start()
 
     def a_edges(i, drain=False):
         @pl.when(both(z == i, z < nz - 1))
         def _():
+            if not drain:
+                own_late(1)
             a_own(1, drain)
 
         @pl.when(both(nz - 1 - z == i, z > 0))
         def _():
+            if not drain:
+                own_late(-1)
             a_own(-1, drain)
 
     def a_sibling(drain=False):
@@ -260,16 +339,14 @@
         ref = cbuf.at[pl.ds(zz * tpp, tpp)]
         return remote(ref, ref, c_send, c_recv, peer, me)
 
-    def owner_of(zz):
-        return lax.div(zz * tpp, gpp)
-
     def share(drain=False):
-        zz = turn(nz - 1)
-
-        @pl.when(owner_of(zz) == k)
-        def _():
-            for other in range(1, states):
-                act(c_copy(zz, lax.rem(k + other, states)), drain)
+        for other in range(1, states):
+            peer = lax.rem(k + other, states)
+            zz = turn_of(peer, nz - 2)
+
+            @pl.when(owner_of(zz) == k)
+            def _():
+                act(c_copy(zz, peer), drain)
 
 
     def p_copy(g, part_of, peer):
@@ -300,25 +377,26 @@
         here = cbuf[g].reshape(pairs * w, TILE).astype(jnp.float32)
         line[kk] += jnp.sum((whole * here).reshape(pairs * w // 8, 8, TILE), axis=0)
 
-    def p_wait(j, use):
-        zz = turn(j)
-
-        @pl.when(owner_of(zz) == k)
-        def _():
-            first = lax.rem(zz * tpp, gpp)
+    def p_wait(use):
+        for i in range(nz // states):
+            zz = k * (nz // states) + i
             for other in range(1, states):
                 peer = lax.rem(k + other, states)
-                ref = precv.at[peer, pl.ds(first, tpp)]
-                remote(ref, ref, p_send, p_recv.at[peer, zz], peer, me).wait_recv()
-                if use:
-                    @pl.loop(0, tpp)
-                    def _(r):
-                        tally(peer, zz * tpp + r, flat_of(peer, first + r))
+                counted = zz == turn_of(peer, nz - 2)
+
+                @pl.when(jnp.logical_not(counted) if use else counted)
+                def _():
+                    ref = precv.at[peer, pl.ds(i * tpp, tpp)]
+                    remote(ref, ref, p_send, p_recv.at[peer, zz], peer, me).wait_recv()
+                    if use:
+                        @pl.loop(0, tpp)
+                        def _(r):
+                            tally(peer, zz * tpp + r, flat_of(peer, i * tpp + r))
 
     def project(j):
         zz = turn(j)
 
-        if j == nz - 1:
+        if j == nz - 2:
             @pl.when(owner_of(zz) != k)
             def _():
                 c_copy(zz, k).wait_recv()
@@ -355,7 +433,7 @@
             whole = prod[: pairs * w]
             owner = lax.div(g, gpp)
 
-            @pl.when(jnp.logical_or(owner == k, j == nz - 1))
+            @pl.when(jnp.logical_or(owner == k, j == nz - 2))
             def _():
                 tally(k, g, whole)
 
@@ -522,7 +600,7 @@
 
     def penalize():
         gathered(2)
-        p_wait(nz - 1, False)
+        p_wait(False)
         scale = 1.0 / (phys * width)
         factors = [weight_ref[kk] * (jnp.sum(istate[:, kk]) * scale) for kk in range(states)]
         for g in range(gpp):
@@ -534,12 +612,24 @@
     line[...] = jnp.zeros_like(line)
     e_load.wait()
     for i in range(nz + 1):
+        if i == 0:
+            own()
+            a_load.wait()
+            unpack()
+            a_first()
+            a_sibling()
+        elif i < nz:
+            if i < nz - 1:
+                natural(i, False)
+            if i == nz - 2:
+                natural(nz - 1, False, range(PARTS - 1))
+                deferred()
+            if i == nz - 1:
+                natural(nz - 1, False, [PARTS - 1])
+            natural(i, True)
+            if i == nz - 1:
+                delayed()
         if i < nz:
-            column(i)
-            if i == 0:
-                a_load.wait()
-                unpack()
-                a_sibling()
             a_edges(i)
             if i == 0:
                 for copy in c_loads:
@@ -549,6 +639,10 @@
             for j in range(nz - 2):
                 for u in range(1, ny):
                     my_copy(turn(j), lax.rem(y + u, ny)).start()
+
+            @pl.loop(0, nch)
+            def _(h):
+                a_pass(h, 1)
         if i >= 1:
             across(i - 1)
             sibling(i - 1)
@@ -556,13 +650,9 @@
                 for copy in loads:
                     copy.wait()
             project(i - 1)
-            if i < nz:
-                for n in range(slices - (i == nz - 1)):
+            if i - 1 < nz - 2:
+                for n in range(slices):
                     hand_over(i - 1, n)
-        if i == nz - 1:
-            @pl.loop(0, nch)
-            def _(h):
-                a_pass(h, 1)
 
     for i in range(2, nz):
         @pl.loop(0, nch)
@@ -571,13 +661,15 @@
 
     for j in range(nz):
         forward(j)
-        if 1 <= j < nz - 1:
-            @pl.loop(0, nch)
-            def _(h):
-                a_last(h, j)
+    p_wait(True)
+    overlap(0)
+    rows_sent()
     for i in range(nz):
-        column(i, drain=True)
         across(i, drain=True)
+    for i in range(1, nz - 1):
+        @pl.loop(0, nch)
+        def _(h):
+            a_last(h, i)
     a_last(0, nz - 1)
     for other in range(1, states):
         peer = lax.rem(k + other, states)
@@ -591,22 +683,21 @@
 
         @pl.when(h == 0)
         def _():
-            hand_over(nz - 2, slices - 1)
+            overlap(1)
 
         for n in range(slices - 1):
-            @pl.when(h == min(n + 1, nch - 1))
-            def _():
+            @pl.when(h == (min(n, nch - 1) if n < slices - 2 else nch - 1))
+            def _():
+                hand_over(nz - 2, n)
                 hand_over(nz - 1, n)
 
         @pl.when(h < nch - 1)
         def _():
             a_last(h + 1, nz - 1)
 
-        @pl.when(h == max(nch - 2, 0))
+        @pl.when(h == nch - 1)
         def _():
-            for j in range(nz - 1):
-                p_wait(j, True)
-            overlap(0)
+            overlap(2)
 
         if direct:
             @pl.when(h > 1)
@@ -615,24 +706,22 @@
 
     if direct:
         pass_on(0)
-        overlap(1)
         finish(nch - 2)
+        hand_over(nz - 2, slices - 1)
+        hand_over(nz - 1, slices - 1)
         for h in range(1, nch - 2):
             pass_on(h)
         finish(nch - 1)
-        hand_over(nz - 1, slices - 1)
-        overlap(2)
         for h in range(max(nch - 2, 1), nch):
             pass_on(h)
     else:
+        hand_over(nz - 2, slices - 1)
         hand_over(nz - 1, slices - 1)
-        overlap(1)
+
 
         @pl.loop(0, mine)
         def _(zc):
             finish(zc)
-
-        overlap(2)
 
         @pl.loop(0, mine)
         def _(zc):

time: 98.2 us -> 96.7 us (0.985)
  Pallas kernels: 95.1 us -> 93.8 us
    pallas_call x1, Pallas kernels: 95.1 us -> 93.8 us  [shards(): pl.pallas_call(functools.partial(kernel, states, bonds, ny, fch), out_sha...]
where the time goes in v4:
time: 96.7 us; the launch traced here: 96.5 us
  Pallas kernels  93.8 us (97%)
  local copies, waits for them, and re-layouts  2.11 us (2%)
    pallas_call x1, Pallas kernels, shards(): pl.pallas_call(functools.partial(kernel, states, bonds, ny, fch), out_sha...  93.8 us
    unnamed x2, local copies, waits for them, and re-layouts  2.11 us

profile of v4, /device:TPU:25, one launch (start us, length us, event | category | flops | bytes accessed | tf_op | source)
XLA Modules:
  0.0 96.5 jit_solution(10333963960410772205)
XLA Ops:
  0.6 93.8 %shard_map.77 = (f32[4,128,1024]{2,1,0:T(8,128)S(1)}, bf16[128,2048]{1,0:T(8,128)(2,1)S(1)}) custom-call(bf16[2,64,2048]{2,1,0:T(8,128)(2,1)} %bitcast.7, bf16[4,128,2048]{2,1,0:T(8,128)(2,1)} %bitcast.5, bf16[2,128,2048]{2,1,0:T(8,128)(2,1)} %bitcast.6, bf16[128,2,1024]{2,1,0:T(2,128)(2,1)} %grow_hbm.1, bf16[4,128,1024]{2,1,0:T(8,128)(2,1)} %current_hbm.1, ...), custom_call_target="tpu_custom_call" | custom-call | tf_op jit(solution)/shard_map/pallas_call | solution.py:795
  94.4 1.3 %copy.10 = f32[4,128,1024]{2,1,0:T(8,128)} copy(f32[4,128,1024]{2,1,0:T(8,128)S(1)} %get-tuple-element.6) | data formatting | bytes 4194304
  95.7 0.8 copy.11

commit v5 on v4

--- a/solution.py
+++ b/solution.py
@@ -466,34 +466,64 @@
                 act(mx_copy(zz, yy, lax.rem(k + other, states)), drain)
 
 
-    def t_copy(zc, yy):
+    def t_copy(zc, yy, kk):
         return remote(
-            part.at[zc, yy], prt.at[zc, y], t_send, t_recv.at[zc, y], k, slot(z, yy, c)
+            part.at[zc, yy, kk], prt.at[zc, y, kk], t_send, t_recv.at[zc, y, kk], k, slot(z, yy, c)
         )
 
-    def grow(h):
+    def parts_of(h):
+        for q in range(bpc):
+            if direct:
+                yield q, h, q
+            else:
+                fb = h * bpc + q
+                yield (
+                    q,
+                    lax.div(fb, ny * nc) * nc + lax.rem(fb, nc),
+                    lax.rem(lax.div(fb, nc), ny),
+                )
+
+    def store(zc, yy, kk, block):
+        @pl.when(yy == y)
+        def _():
+            acc[zc, kk] = block
+
+        @pl.when(yy != y)
+        def _():
+            part[zc, yy, kk] = block.astype(jnp.bfloat16)
+
+    def grow(h, kk):
+        total = jnp.dot(
+            mbuf[kk].reshape(ny * w, nz * piece),
+            abuf[h].reshape(nz * piece, fch),
+            preferred_element_type=jnp.float32,
+        )
+        for q, zc, yy in parts_of(h):
+            store(zc, yy, kk, total[:, q * w : (q + 1) * w])
+
+            @pl.when(yy != y)
+            def _():
+                t_copy(zc, yy, kk).start()
+
+    def grow_all(h):
         total = jnp.dot(
             mbuf[...].reshape(ecols, nz * piece),
             abuf[h].reshape(nz * piece, fch),
             preferred_element_type=jnp.float32,
         )
-        for q in range(bpc):
-            if direct:
-                zc, yy = h, q
-            else:
-                fb = h * bpc + q
-                zc = lax.div(fb, ny * nc) * nc + lax.rem(fb, nc)
-                yy = lax.rem(lax.div(fb, nc), ny)
-            block = total[:, q * w : (q + 1) * w]
-
-            @pl.when(yy == y)
-            def _():
-                acc[zc] = block
+        for q, zc, yy in parts_of(h):
+            for kk in range(states):
+                store(zc, yy, kk, total[kk * ny * w : (kk + 1) * ny * w, q * w : (q + 1) * w])
 
             @pl.when(yy != y)
             def _():
-                part[zc, yy] = block.astype(jnp.bfloat16)
-                t_copy(zc, yy).start()
+                for other in range(1, states + 1):
+                    t_copy(zc, yy, lax.rem(k + other, states)).start()
+
+    def grow_others(h):
+        @pl.loop(1, states)
+        def _(other):
+            grow(h, lax.rem(k + other, states))
 
     def target(kk, zc):
         return slot(kk * (nz // states) + lax.div(zc, nc), y, lax.rem(zc, nc))
@@ -524,30 +554,26 @@
     def r_copy(kk, zc):
         return remote(nsend.at[kk, zc], nbuf.at[k, zc], r_send, r_recv.at[k, zc], kk, me)
 
-    def finish(zc):
-        total = acc[zc]
+    def summed(zc, kk):
+        total = acc[zc, kk]
         for u in range(1, ny):
             yy = lax.rem(y + u, ny)
-            ref = prt.at[zc, yy]
-            remote(ref, ref, t_send, t_recv.at[zc, yy], k, me).wait_recv()
+            ref = prt.at[zc, yy, kk]
+            remote(ref, ref, t_send, t_recv.at[zc, yy, kk], k, me).wait_recv()
             total = total + ref[...].astype(jnp.float32)
-        for kk in range(states):
-            blocks = [
-                total[(kk * ny + yy) * w : (kk * ny + yy + 1) * w].T.astype(jnp.bfloat16)
-                for yy in range(ny)
-            ]
-
-            @pl.when(kk == k)
-            def _():
-                for yy in range(ny):
-                    nbuf[k, zc, yy] = blocks[yy]
-                deliver(k, zc)
-
-            @pl.when(kk != k)
-            def _():
-                for yy in range(ny):
-                    nsend[kk, zc, yy] = blocks[yy]
-                r_copy(kk, zc).start()
+        return [total[yy * w : (yy + 1) * w].T.astype(jnp.bfloat16) for yy in range(ny)]
+
+    def finish(zc):
+        for other in range(1, states):
+            kk = lax.rem(k + other, states)
+            blocks = summed(zc, kk)
+            for yy in range(ny):
+                nsend[kk, zc, yy] = blocks[yy]
+            r_copy(kk, zc).start()
+        blocks = summed(zc, k)
+        for yy in range(ny):
+            nbuf[k, zc, yy] = blocks[yy]
+        deliver(k, zc)
 
     def pass_on(zc):
         for other in range(1, states):
@@ -671,39 +697,41 @@
         def _(h):
             a_last(h, i)
     a_last(0, nz - 1)
+
+    a_ready(0)
+    grow(0, k)
+
     for other in range(1, states):
         peer = lax.rem(k + other, states)
         ref = mbuf.at[peer]
         remote(ref, ref, mx_send, mx_recv.at[peer], peer, me).wait_recv()
 
-    @pl.loop(0, nch)
+    grow_others(0)
+    overlap(1)
+    for n in range(slices - 2):
+        hand_over(nz - 2, n)
+        hand_over(nz - 1, n)
+
+    if nch > 1:
+        a_last(1, nz - 1)
+
+    @pl.loop(1, nch)
     def _(h):
         a_ready(h)
-        grow(h)
-
-        @pl.when(h == 0)
-        def _():
-            overlap(1)
-
-        for n in range(slices - 1):
-            @pl.when(h == (min(n, nch - 1) if n < slices - 2 else nch - 1))
-            def _():
-                hand_over(nz - 2, n)
-                hand_over(nz - 1, n)
+        grow_all(h)
 
         @pl.when(h < nch - 1)
         def _():
             a_last(h + 1, nz - 1)
 
-        @pl.when(h == nch - 1)
-        def _():
-            overlap(2)
-
         if direct:
             @pl.when(h > 1)
             def _():
                 finish(h - 2)
 
+    hand_over(nz - 2, slices - 2)
+    hand_over(nz - 1, slices - 2)
+    overlap(2)
     if direct:
         pass_on(0)
         finish(nch - 2)
@@ -758,7 +786,8 @@
     @pl.loop(0, mine)
     def _(zc):
         for u in range(1, ny):
-            t_copy(zc, lax.rem(y + u, ny)).wait_send()
+            for kk in range(states):
+                t_copy(zc, lax.rem(y + u, ny), kk).wait_send()
         for kk in range(states):
             @pl.when(kk != k)
             def _():
@@ -810,9 +839,9 @@
             pltpu.VMEM((states, gpp, PARTS, pairs * w // PARTS, TILE), bf),
             pltpu.VMEM((nz, ny, w, piece), bf),
             pltpu.VMEM((states, ny, w, nz * piece), bf),
-            pltpu.VMEM((mine, states * ny * w, w), f32),
-            pltpu.VMEM((mine, ny, states * ny * w, w), bf),
-            pltpu.VMEM((mine, ny, states * ny * w, w), bf),
+            pltpu.VMEM((mine, states, ny * w, w), f32),
+            pltpu.VMEM((mine, ny, states, ny * w, w), bf),
+            pltpu.VMEM((mine, ny, states, ny * w, w), bf),
             pltpu.VMEM((states, mine, ny, w, w), bf),
             pltpu.VMEM((states, mine, ny, w, w), bf),
             pltpu.VMEM((CORES * ny, states, 128), f32),
@@ -827,7 +856,7 @@
             dma, dma((states,)),
             dma, dma,
             dma((3,)), dma((3,)),
-            dma, dma((mine, ny)),
+            dma, dma((mine, ny, states)),
             dma, dma((states, mine)),
             dma, dma,
         ],

time: 96.7 us -> 95.5 us (0.988)
  Pallas kernels: 93.8 us -> 92.6 us
    pallas_call x1, Pallas kernels: 93.8 us -> 92.6 us  [shards(): pl.pallas_call(functools.partial(kernel, states, bonds, ny, fch), out_sha...]
where the time goes in v5:
time: 95.5 us; the launch traced here: 95.4 us
  Pallas kernels  92.6 us (97%)
  local copies, waits for them, and re-layouts  2.11 us (2%)
    pallas_call x1, Pallas kernels, shards(): pl.pallas_call(functools.partial(kernel, states, bonds, ny, fch), out_sha...  92.6 us
    unnamed x2, local copies, waits for them, and re-layouts  2.11 us

profile of v5, /device:TPU:25, one launch (start us, length us, event | category | flops | bytes accessed | tf_op | source)
XLA Modules:
  0.0 95.4 jit_solution(9260027242850706221)
XLA Ops:
  0.6 92.6 %shard_map.77 = (f32[4,128,1024]{2,1,0:T(8,128)S(1)}, bf16[128,2048]{1,0:T(8,128)(2,1)S(1)}) custom-call(bf16[2,64,2048]{2,1,0:T(8,128)(2,1)} %bitcast.7, bf16[4,128,2048]{2,1,0:T(8,128)(2,1)} %bitcast.5, bf16[2,128,2048]{2,1,0:T(8,128)(2,1)} %bitcast.6, bf16[128,2,1024]{2,1,0:T(2,128)(2,1)} %grow_hbm.1, bf16[4,128,1024]{2,1,0:T(8,128)(2,1)} %current_hbm.1, ...), custom_call_target="tpu_custom_call" | custom-call | tf_op jit(solution)/shard_map/pallas_call | solution.py:824
  93.3 1.3 %copy.10 = f32[4,128,1024]{2,1,0:T(8,128)} copy(f32[4,128,1024]{2,1,0:T(8,128)S(1)} %get-tuple-element.6) | data formatting | bytes 4194304
  94.6 0.8 copy.11

commit v6 on v5

--- a/solution.py
+++ b/solution.py
@@ -649,6 +649,8 @@
                 natural(i, False)
             if i == nz - 2:
                 natural(nz - 1, False, range(PARTS - 1))
+                for u in range(1, ny):
+                    my_copy(turn(0), lax.rem(y + u, ny)).start()
                 deferred()
             if i == nz - 1:
                 natural(nz - 1, False, [PARTS - 1])
@@ -662,7 +664,7 @@
                     copy.wait()
                 share()
         if i == nz - 1:
-            for j in range(nz - 2):
+            for j in range(1, nz - 2):
                 for u in range(1, ny):
                     my_copy(turn(j), lax.rem(y + u, ny)).start()
 
@@ -676,6 +678,8 @@
                 for copy in loads:
                     copy.wait()
             project(i - 1)
+            if i == nz - 1:
+                forward(0)
             if i - 1 < nz - 2:
                 for n in range(slices):
                     hand_over(i - 1, n)
@@ -685,7 +689,7 @@
         def _(h):
             a_pass(h, i)
 
-    for j in range(nz):
+    for j in range(1, nz):
         forward(j)
     p_wait(True)
     overlap(0)

time: 95.5 us -> 95.5 us (level)
  no operation moved by 1% of the time
where the time goes in v6:
time: 95.5 us; the launch traced here: 95.4 us
  Pallas kernels  92.6 us (97%)
  local copies, waits for them, and re-layouts  2.11 us (2%)
    pallas_call x1, Pallas kernels, shards(): pl.pallas_call(functools.partial(kernel, states, bonds, ny, fch), out_sha...  92.6 us
    unnamed x2, local copies, waits for them, and re-layouts  2.11 us

profile of v6, /device:TPU:25, one launch (start us, length us, event | category | flops | bytes accessed | tf_op | source)
XLA Modules:
  0.0 95.4 jit_solution(12731040128315842446)
XLA Ops:
  0.6 92.6 %shard_map.77 = (f32[4,128,1024]{2,1,0:T(8,128)S(1)}, bf16[128,2048]{1,0:T(8,128)(2,1)S(1)}) custom-call(bf16[2,64,2048]{2,1,0:T(8,128)(2,1)} %bitcast.7, bf16[4,128,2048]{2,1,0:T(8,128)(2,1)} %bitcast.5, bf16[2,128,2048]{2,1,0:T(8,128)(2,1)} %bitcast.6, bf16[128,2,1024]{2,1,0:T(2,128)(2,1)} %grow_hbm.1, bf16[4,128,1024]{2,1,0:T(8,128)(2,1)} %current_hbm.1, ...), custom_call_target="tpu_custom_call" | custom-call | tf_op jit(solution)/shard_map/pallas_call | solution.py:828
  93.3 1.3 %copy.10 = f32[4,128,1024]{2,1,0:T(8,128)} copy(f32[4,128,1024]{2,1,0:T(8,128)S(1)} %get-tuple-element.6) | data formatting | bytes 4194304
  94.6 0.8 copy.11
